TPU v7x, 128 devices: a whole 4x4x4 slice. The times are simulated.
128 devices in a mesh: grid: 16 (over y, z_lo, core), dom: 8 (over x, z_hi).
Axes of the slice: x: 4, y: 4, z: 4 (z_hi: 2, z_lo: 2; z = z_hi * 2 + z_lo), core: 2. Of those that a mesh axis runs over, the one named last changes fastest.
Arguments:
- values: float32 [16, 32, 4, 4, 8, 8, 128], P('grid', 'dom'), may hold values from -2 to 2
- levels: int32 [16, 6], P('grid'), may hold values from 0 to 7, as said below
- coefficients: int32 [16], P('grid'), may hold values from -3 to 3, as said below
Outputs:
- combined: float32 [16, 32, 4, 4, 8, 8, 128], P('grid', 'dom')
Inputs may be any that keep to these rules, and one draw needn't show every extreme that they name: levels[g, k] is grid g's level along dimension k + 1. With L_k the base-two logarithm of that dimension's extent (32, 4, 4, 8, 8, 128), each entry lies between L_k - 2 and L_k, and the shortfalls L_k - levels[g, k] of one grid add up to 2 at most. `coefficients`: every coefficient is nonzero.
All inputs are finite; a program needn't handle non-finite values.
Results may differ from a plain program's by a relative error of at most 0.0003.
Values sent between devices are 32-bit elements; how exact they have to be, the bound alone decides.
No kernel may reach another device: no remote copies, remote signals or barrier semaphores. Data moves between devices by JAX's collectives and lax.ppermute only.
A program may use at most 64 MiB of HBM per device.

v0:
```python
import jax
import jax.numpy as jnp
import numpy as np
from jax import lax
from jax.sharding import PartitionSpec as P

PRECISE = lax.Precision.HIGHEST


def cut_along(x, dim, peers):
    before, after = (x.shape[:dim], x.shape[dim + 1 :])
    return jnp.moveaxis(x.reshape(*before, peers, -1, *after), dim, 0)


def sent_and_summed(x, axis, dim):
    parts = cut_along(x, dim, lax.axis_size(axis))
    arrived = lax.all_to_all(parts, axis, split_axis=0, concat_axis=0, tiled=True)
    return arrived.sum(axis=0)


def laid_out(parts, dim):
    parts = jnp.moveaxis(parts, 0, dim)
    shape = parts.shape
    return parts.reshape(*shape[:dim], shape[dim] * shape[dim + 1], *shape[dim + 2 :])


def from_everyone(x, axis):
    copies = jnp.broadcast_to(x, (lax.axis_size(axis), *x.shape))
    return lax.all_to_all(copies, axis, split_axis=0, concat_axis=0, tiled=True)


def collect(x, axis, dim):
    return laid_out(from_everyone(x, axis), dim)


def coarse_position(numerator, level_now):
    while numerator > 0 and numerator % 2 == 0:
        numerator = numerator // 2
        level_now = level_now - 1
    if numerator == 0:
        return 0
    return (1 << level_now - 1) + (numerator - 1) // 2


def parent_positions(position):
    level_now = position.bit_length()
    span_size = 1 << level_now - 1
    offset = position - span_size
    return [
        coarse_position(offset % span_size, level_now - 1),
        coarse_position((offset + 1) % span_size, level_now - 1),
    ]


def hier_table(points):
    matrix = np.eye(points)
    for position in range(1, points):
        for parent in parent_positions(position):
            matrix[position, parent] -= 0.5
    return matrix


def dehier_table(points):
    matrix = np.zeros((points, points))
    matrix[0, 0] = 1.0
    for position in range(1, points):
        row_now = np.zeros(points)
        row_now[position] = 1.0
        for parent in parent_positions(position):
            row_now = row_now + 0.5 * matrix[parent]
        matrix[position] = row_now
    return matrix


def nodal_order(points):
    placed = np.zeros(points, dtype=np.int64)
    for position in range(1, points):
        level_now = position.bit_length()
        offset = position - (1 << level_now - 1)
        placed[position] = (2 * offset + 1) * points // (1 << level_now)
    return placed


def nodal_table(matrix):
    placed = nodal_order(matrix.shape[0])
    result = np.zeros(matrix.shape)
    result[placed[:, None], placed[None, :]] = matrix
    return result


def local_hier(points):
    matrix = np.zeros((points, points + 1))
    matrix[0, 0] = 1.0
    for point in range(1, points):
        stride = point & -point
        matrix[point, point] = 1.0
        matrix[point, point - stride] -= 0.5
        matrix[point, point + stride] -= 0.5
    return matrix


def local_dehier(points):
    matrix = np.zeros((points + 1, points + 1))
    matrix[0, 0] = 1.0
    matrix[points, points] = 1.0
    stride = points // 2
    while stride >= 1:
        for point in range(stride, points, 2 * stride):
            row_now = np.zeros(points + 1)
            row_now[point] = 1.0
            matrix[point] = row_now + 0.5 * (matrix[point - stride] + matrix[point + stride])
        stride = stride // 2
    return matrix[:points]


def apply_table(grid_data, matrix, dim_index):
    letters = "abcdefg"[: grid_data.ndim]
    outputs = letters[:dim_index] + "z" + letters[dim_index + 1 :]
    formula = letters + ",z" + letters[dim_index] + "->" + outputs
    return jnp.einsum(formula, grid_data, jnp.asarray(matrix, dtype=jnp.float32), precision=PRECISE)


def tail_column(column, rank_count):
    return jnp.asarray(column, dtype=jnp.float32).reshape((-1,) + (1,) * (rank_count - 1))


def holding_mask(level_row, extents):
    holding = jnp.ones(extents, dtype=jnp.float32)
    for dim_index, points in enumerate(extents):
        limit = jnp.left_shift(jnp.int32(1), level_row[dim_index])
        inside = (jnp.arange(points, dtype=jnp.int32) < limit).astype(jnp.float32)
        shape_now = [1] * len(extents)
        shape_now[dim_index] = points
        holding = holding * inside.reshape(shape_now)
    return holding


def split_rows_mask(level_count, local_rows, rank_count):
    members = lax.axis_size("dom")
    total_rows = local_rows * members
    rows_here = lax.axis_index("dom") * local_rows + jnp.arange(local_rows, dtype=jnp.int32)
    spacing = jnp.right_shift(jnp.int32(total_rows), level_count)
    inside = (jnp.remainder(rows_here, spacing) == 0).astype(jnp.float32)
    return inside.reshape((local_rows,) + (1,) * (rank_count - 1))


def split_hierarchize(grid_data):
    members = lax.axis_size("dom")
    own_index = lax.axis_index("dom")
    first_row = grid_data[0]
    all_firsts = lax.all_gather(first_row[None], "dom", axis=0, tiled=True)
    coarse = apply_table(all_firsts, nodal_table(hier_table(members)), 0)
    new_first = lax.dynamic_index_in_dim(coarse, own_index, 0, keepdims=False)
    following = lax.dynamic_index_in_dim(all_firsts, (own_index + 1) % members, 0, keepdims=False)
    local_rows = grid_data.shape[0]
    matrix = local_hier(local_rows)
    result = (
        apply_table(grid_data, matrix[:, :local_rows], 0)
        + tail_column(matrix[:, local_rows], grid_data.ndim) * following[None]
    )
    return result.at[0].set(new_first)


def split_dehierarchize(grid_data):
    members = lax.axis_size("dom")
    own_index = lax.axis_index("dom")
    first_row = grid_data[0]
    all_firsts = lax.all_gather(first_row[None], "dom", axis=0, tiled=True)
    coarse = apply_table(all_firsts, nodal_table(dehier_table(members)), 0)
    new_first = lax.dynamic_index_in_dim(coarse, own_index, 0, keepdims=False)
    following = lax.dynamic_index_in_dim(coarse, (own_index + 1) % members, 0, keepdims=False)
    local_rows = grid_data.shape[0]
    grid_data = grid_data.at[0].set(new_first)
    matrix = local_dehier(local_rows)
    return (
        apply_table(grid_data, matrix[:, :local_rows], 0)
        + tail_column(matrix[:, local_rows], grid_data.ndim) * following[None]
    )


def body(values, levels, coefficients):
    grid_data = values[0]
    level_row = levels[0]
    weight = coefficients[0].astype(jnp.float32)
    extents = tuple(grid_data.shape[1:])
    local_rows = grid_data.shape[0]
    for dim_index in range(1, 6):
        grid_data = apply_table(grid_data, hier_table(grid_data.shape[dim_index]), dim_index)
    grid_data = split_hierarchize(grid_data)
    holding = (
        split_rows_mask(level_row[0], local_rows, grid_data.ndim)
        * holding_mask(level_row[1:], extents)[None]
    )
    weighted = weight * holding * grid_data
    merged = weighted.reshape((local_rows, extents[0] * extents[1]) + extents[2:])
    own_share = sent_and_summed(merged, "grid", 1)
    for dim_index in range(2, 5):
        own_share = apply_table(own_share, dehier_table(own_share.shape[dim_index]), dim_index)
    own_share = split_dehierarchize(own_share)
    gathered = collect(own_share, "grid", 1)
    combined = gathered.reshape(grid_data.shape)
    for dim_index in range(1, 3):
        combined = apply_table(combined, dehier_table(extents[dim_index - 1]), dim_index)
    return (holding * combined)[None]


def solution(mesh):
    in_specs = (P("grid", "dom", None, None, None, None, None), P("grid", None), P("grid"))
    out_specs = P("grid", "dom", None, None, None, None, None)
    return jax.shard_map(body, mesh=mesh, in_specs=in_specs, out_specs=out_specs, check_vma=False)
```

profile of v0, /device:TPU:1, one launch (start us, length us, event | category | flops | bytes accessed | tf_op | source)
XLA Modules:
  0.0 251.5 jit_solution(10346107945402557805)
XLA Ops:
  6.5 1.6 copy-done
  8.1 5.0 %fusion.20 = f32[4,4,4,8,8,128]{5,1,4,3,2,0:T(4,128)S(1)} fusion(f32[4,4,1,1,1,1]{1,0,5,4,3,2:T(4,128)} %constant.147, f32[4,4,4,8,8,128]{5,4,3,2,1,0:T(8,128)S(1)} %bitcast.96), kind=kOutput, calls=%fused_computation.24 | convolution fusion | flops 25165824 | bytes 4194368 | tf_op jit(solution)/shard_map/abcdef,zb->azcdef/dot_general | solution.py:120
  13.2 4.5 %fusion.23 = f32[4,4,4,8,8,128]{5,2,4,3,1,0:T(4,128)S(1)} fusion(f32[4,4,1,1,1,1]{1,0,5,4,3,2:T(4,128)S(1)} %copy-done.9, f32[4,4,4,8,8,128]{5,1,4,3,2,0:T(4,128)S(1)} %fusion.20), kind=kOutput, calls=%fused_computation.25 | convolution fusion | flops 25165824 | bytes 4194368 | tf_op jit(solution)/shard_map/abcdef,zc->abzdef/dot_general | solution.py:120
  17.7 3.0 %fusion.26 = f32[4,4,4,8,8,128]{5,3,4,2,1,0:T(8,128)S(1)} fusion(f32[8,8,1,1,1,1]{1,0,5,4,3,2:T(8,128)S(1)} %copy-done.7, f32[4,4,4,8,8,128]{5,2,4,3,1,0:T(4,128)S(1)} %fusion.23), kind=kOutput, calls=%fused_computation.26 | convolution fusion | flops 50331648 | bytes 4194560 | tf_op jit(solution)/shard_map/abcdef,zd->abczef/dot_general | solution.py:120
  20.8 2.1 fusion.12
  22.9 1.9 fusion.6
  24.8 1.3 copy-done.1
  26.1 0.8 slice.114
  27.7 0.7 fusion.39
  32.5 68.7 %all-gather.3.cloned.1.call-done = f32[8,4,4,8,8,128]{5,4,3,2,1,0:T(8,128)} async-done(((f32[1,4,4,8,8,128]{5,4,3,2,1,0:T(8,128)}), f32[8,4,4,8,8,128]{5,4,3,2,1,0:T(8,128)}) %all-gather.3.cloned.1.call-update) | async-done | bytes 4194320 | tf_op jit(solution)/shard_map/all_gather | solution.py:151
  101.2 8.1 %fusion = f32[4,4,8,8,128,8]{4,5,3,2,1,0:T(8,128)S(1)} fusion(f32[8,8,1,1,1,1]{1,0,5,4,3,2:T(8,128)S(1)} %copy-done.11, f32[8,4,4,8,8,128]{5,4,3,2,1,0:T(8,128)} %all-gather.3.cloned.1.call-done), kind=kOutput, calls=%fused_computation | convolution fusion | flops 100663296 | bytes 8388864 | tf_op jit(solution)/shard_map/abcdef,za->zbcdef/dot_general | solution.py:120
  109.4 0.6 dynamic-slice_bitcast_fusion
  110.0 1.1 dynamic-slice_bitcast_fusion.1
  111.1 5.7 %multiply_add_fusion = f32[4,4,4,8,8,128]{5,0,4,3,2,1:T(4,128)} fusion(f32[4,4,1,1,1,1]{1,0,5,4,3,2:T(4,128)S(1)} %copy-done.13, f32[4,4,4,8,8,128]{5,4,3,2,1,0:T(8,128)S(1)} %copy-done.2, f32[4,4,8,8,128]{4,3,2,1,0:T(8,128)S(1)} %dynamic-slice_bitcast_fusion.1, f32[4]{0:T(128)S(1)} %copy-done.15), kind=kOutput, calls=%fused_computation.23 | convolution fusion | flops 26214400 | bytes 4718672 | tf_op jit(solution)/shard_map/abcdef,za->zbcdef/dot_general | solution.py:120
  116.8 13.8 %scatter.6 = f32[4,4,4,8,8,128]{5,0,4,3,2,1:T(4,128)} dynamic-update-slice(f32[4,4,4,8,8,128]{5,0,4,3,2,1:T(4,128)} %multiply_add_fusion, f32[1,4,4,8,8,128]{5,0,4,3,2,1:T(1,128)S(1)} %dynamic-slice_bitcast_fusion, s32[]{:T(128)} %constant.123.clone.1, s32[]{:T(128)} %constant.123.clone.1, s32[]{:T(128)} %constant.123.clone.1, s32[]{:T(128)} %constant.123.clone.1, s32[]{:T(128)} %constant.123.clone.1, ...) | dynamic-update-slice | bytes 1048580 | tf_op jit(solution)/shard_map/scatter | solution.py:161
  130.6 2.3 fusion.2
  133.0 32.1 %all_to_all.10 = f32[16,4,1,8,8,128]{5,1,4,3,2,0:T(4,128)S(1)} all-to-all(f32[16,4,1,8,8,128]{5,1,4,3,2,0:T(4,128)S(1)} %bitcast.97), channel_id=1, replica_groups=mesh['grid'=16,'dom'=8] {'grid'}, dimensions={0} | all-to-all | bytes 4194304 | tf_op jit(solution)/shard_map/all_to_all | solution.py:17
  166.7 28.1 %all-gather = f32[8,8,8,128]{3,2,1,0:T(8,128)S(1)} all-gather(f32[1,8,8,128]{3,2,1,0:T(8,128)S(1)} %slice.115), channel_id=2, replica_groups=mesh['grid'=16,'dom'=8] {'dom'}, dimensions={0}, use_global_device_ids=true | all-gather | bytes 294912 | tf_op jit(solution)/shard_map/all_gather | solution.py:168
  194.8 0.5 fusion.34
  196.1 36.6 %all_to_all.11 = f32[16,4,1,8,8,128]{5,4,3,1,2,0:T(8,128)S(1)} all-to-all(f32[16,4,1,8,8,128]{5,4,3,1,2,0:T(8,128)S(1)} %broadcast_in_dim.4), channel_id=1, replica_groups=mesh['grid'=16,'dom'=8] {'grid'}, dimensions={0} | all-to-all | bytes 4194304 | tf_op jit(solution)/shard_map/all_to_all | solution.py:29
  232.7 4.3 %fusion.31 = f32[4,4,4,8,8,128]{5,1,4,3,2,0:T(4,128)S(1)} fusion(f32[4,4,1,1,1,1]{1,0,5,4,3,2:T(4,128)S(1)} %copy-done.8, f32[4,4,4,8,8,128]{5,4,3,0,2,1:T(8,128)S(1)} %bitcast.98), kind=kOutput, calls=%fused_computation.27 | convolution fusion | flops 25165824 | bytes 4194368 | tf_op jit(solution)/shard_map/abcdef,zb->azcdef/dot_general | solution.py:120
  237.0 4.3 %fusion.8 = f32[4,4,8,8,128,4]{4,5,3,2,1,0:T(4,128)S(1)} fusion(f32[4,4,1,1,1,1]{1,0,5,4,3,2:T(4,128)S(1)} %copy-done.8, f32[4,4,4,8,8,128]{5,1,4,3,2,0:T(4,128)S(1)} %fusion.31), kind=kOutput, calls=%fused_computation.11 | convolution fusion | flops 25165824 | bytes 4194368 | tf_op jit(solution)/shard_map/abcdef,zc->abzdef/dot_general | solution.py:120
  241.4 1.6 fusion.3
  243.0 1.6 copy.89
  (47 shorter events, 2.6 us)
Async XLA Ops:
  6.5 1.6 copy-start
  6.5 94.7 %all-gather.3.cloned.1.call-start = ((), (), s32[]{:S(2)}) async-start(), calls=%async_computation.2 | async-start | bytes 4718592 | tf_op jit(solution)/shard_map/all_gather | solution.py:151
  8.1 5.0 %copy-start.9 = (f32[4,4,1,1,1,1]{1,0,5,4,3,2:T(4,128)S(1)}, f32[4,4,1,1,1,1]{1,0,5,4,3,2:T(4,128)}, u32[]{:S(2)}) copy-start(f32[4,4,1,1,1,1]{1,0,5,4,3,2:T(4,128)} %constant.147) | copy-start | bytes 196
  13.2 4.5 %copy-start.7 = (f32[8,8,1,1,1,1]{1,0,5,4,3,2:T(8,128)S(1)}, f32[8,8,1,1,1,1]{1,0,5,4,3,2:T(8,128)}, u32[]{:S(2)}) copy-start(f32[8,8,1,1,1,1]{1,0,5,4,3,2:T(8,128)} %constant.148) | copy-start | bytes 772
  20.7 2.1 copy-start.3
  22.9 4.8 %copy-start.5 = (s32[1,6]{1,0:T(1,128)S(1)}, s32[1,6]{1,0:T(1,128)}, u32[]{:S(2)}) copy-start(s32[1,6]{1,0:T(1,128)} %param.24) | copy-start | bytes 76
  24.8 1.3 copy-start.1
  26.1 75.1 %copy-start.11 = (f32[8,8,1,1,1,1]{1,0,5,4,3,2:T(8,128)S(1)}, f32[8,8,1,1,1,1]{1,0,5,4,3,2:T(8,128)}, u32[]{:S(2)}) copy-start(f32[8,8,1,1,1,1]{1,0,5,4,3,2:T(8,128)} %constant.150) | copy-start | bytes 772
  101.2 9.9 %copy-start.13 = (f32[4,4,1,1,1,1]{1,0,5,4,3,2:T(4,128)S(1)}, f32[4,4,1,1,1,1]{1,0,5,4,3,2:T(4,128)}, u32[]{:S(2)}) copy-start(f32[4,4,1,1,1,1]{1,0,5,4,3,2:T(4,128)} %constant.146) | copy-start | bytes 196
  109.4 1.7 copy-start.2
  109.4 1.7 copy-start.15
  165.1 0.7 copy-start.6
  165.1 1.3 copy-start.4
  165.1 29.7 %copy-start.10 = (f32[8,8,1,1]{1,0,3,2:T(8,128)S(1)}, f32[8,8,1,1]{1,0,3,2:T(8,128)}, u32[]{:S(2)}) copy-start(f32[8,8,1,1]{1,0,3,2:T(8,128)} %constant.152) | copy-start | bytes 772
  165.1 30.3 %copy-start.12 = (f32[4,4,1,1]{1,0,3,2:T(4,128)S(1)}, f32[4,4,1,1]{1,0,3,2:T(4,128)}, u32[]{:S(2)}) copy-start(f32[4,4,1,1]{1,0,3,2:T(4,128)} %constant.144) | copy-start | bytes 196
  165.1 30.3 %copy-start.14 = (f32[4]{0:T(128)S(1)}, f32[4]{0:T(128)}, u32[]{:S(2)}) copy-start(f32[4]{0:T(128)} %constant.139.clone) | copy-start | bytes 52
  196.1 36.6 %copy-start.8 = (f32[4,4,1,1,1,1]{1,0,5,4,3,2:T(4,128)S(1)}, f32[4,4,1,1,1,1]{1,0,5,4,3,2:T(4,128)}, u32[]{:S(2)}) copy-start(f32[4,4,1,1,1,1]{1,0,5,4,3,2:T(4,128)} %constant.153) | copy-start | bytes 196
Sparse Core Ops, SparseCore 0:
  27.1 74.0 all-gather.2
where the time goes:
time: 252 us; the launch traced here: 251 us
  blocking collectives  96.8 us (38%)
  waiting for transfers between devices  68.7 us (27%)
  matrix products  40.8 us (16%)
  local copies, waits for them, and re-layouts  22.3 us (9%)
  between operations  18.2 us (7%)
  other arithmetic  4.6 us (2%)
    all_gather x1, waiting for transfers between devices, split_hierarchize(): all_firsts = lax.all_gather(first_row[None], 'dom', axis=0, tiled=True)  68.7 us
    dot_general x14, matrix products, apply_table(): jnp.einsum(formula, grid_data, jnp.asarray(matrix, dtype=jnp.float32), pr...  40.8 us
    all_to_all x1, blocking collectives, from_everyone(): return lax.all_to_all(copies, axis, split_axis=0, concat_axis=0, tiled=True)  36.6 us
    all_to_all x1, blocking collectives, sent_and_summed(): lax.all_to_all(parts, axis, split_axis=0, concat_axis=0, tiled=True)  32.1 us
    all_gather x1, blocking collectives, split_dehierarchize(): all_firsts = lax.all_gather(first_row[None], 'dom', axis=0, tiled=True)  28.1 us
    scatter x1, local copies, waits for them, and re-layouts, split_hierarchize(): return result.at[0].set(new_first)  13.8 us
  transfers between devices with their start and end apart: 1, of which 1 were waited for; matrix products, arithmetic and copies ran while one was open for 0% of the time, Pallas kernels for 0%

commit v1 on v0

--- a/solution.py
+++ b/solution.py
@@ -148,7 +148,9 @@
     members = lax.axis_size("dom")
     own_index = lax.axis_index("dom")
     first_row = grid_data[0]
-    all_firsts = lax.all_gather(first_row[None], "dom", axis=0, tiled=True)
+    all_firsts = jnp.concatenate(
+        lax.all_to_all(jnp.stack([first_row[None]] * lax.axis_size("dom")), "dom", 0, 0), axis=0
+    )
     coarse = apply_table(all_firsts, nodal_table(hier_table(members)), 0)
     new_first = lax.dynamic_index_in_dim(coarse, own_index, 0, keepdims=False)
     following = lax.dynamic_index_in_dim(all_firsts, (own_index + 1) % members, 0, keepdims=False)

time: 252 us -> 234 us (0.929)
  waiting for transfers between devices: 68.7 us -> 53.5 us
  between operations: 18.2 us -> 4.77 us
  starting transfers between devices: 0.01 us -> 8.28 us
    all_gather x1 -> x0, waiting for transfers between devices: 68.7 us -> none  [split_hierarchize(): all_firsts = lax.all_gather(first_row[None], 'dom', axis=0, tiled=True)]
    all_to_all x0 -> x1, waiting for transfers between devices: none -> 53.5 us  [split_hierarchize(): lax.all_to_all(jnp.stack([first_row[None]] * lax.axis_size('dom')), 'dom'...]
    all_to_all x0 -> x1, starting transfers between devices: none -> 8.28 us  [split_hierarchize(): lax.all_to_all(jnp.stack([first_row[None]] * lax.axis_size('dom')), 'dom'...]
where the time goes in v1:
time: 234 us; the launch traced here: 233 us
  blocking collectives  97.7 us (42%)
  waiting for transfers between devices  53.5 us (23%)
  matrix products  40.6 us (17%)
  local copies, waits for them, and re-layouts  24 us (10%)
  starting transfers between devices  8.28 us (4%)
  between operations  4.77 us (2%)
  other arithmetic  4.6 us (2%)
    all_to_all x1, waiting for transfers between devices, split_hierarchize(): lax.all_to_all(jnp.stack([first_row[None]] * lax.axis_size('dom')), 'dom'...  53.5 us
    dot_general x14, matrix products, apply_table(): jnp.einsum(formula, grid_data, jnp.asarray(matrix, dtype=jnp.float32), pr...  40.6 us
    all_to_all x1, blocking collectives, from_everyone(): return lax.all_to_all(copies, axis, split_axis=0, concat_axis=0, tiled=True)  36.6 us
    all_to_all x1, blocking collectives, sent_and_summed(): lax.all_to_all(parts, axis, split_axis=0, concat_axis=0, tiled=True)  32.9 us
    all_gather x1, blocking collectives, split_dehierarchize(): all_firsts = lax.all_gather(first_row[None], 'dom', axis=0, tiled=True)  28.2 us
    scatter x1, local copies, waits for them, and re-layouts, split_hierarchize(): return result.at[0].set(new_first)  13.8 us
    all_to_all x1, starting transfers between devices, split_hierarchize(): lax.all_to_all(jnp.stack([first_row[None]] * lax.axis_size('dom')), 'dom'...  8.28 us
  transfers between devices with their start and end apart: 1, of which 1 were waited for; matrix products, arithmetic and copies ran while one was open for 0% of the time, Pallas kernels for 0%

profile of v1, /device:TPU:1, one launch (start us, length us, event | category | flops | bytes accessed | tf_op | source)
XLA Modules:
  0.0 233.4 jit_solution(14319497212062075188)
XLA Ops:
  0.0 1.6 copy-done
  1.6 5.0 %fusion.21 = f32[4,4,4,8,8,128]{5,1,4,3,2,0:T(4,128)S(1)} fusion(f32[4,4,1,1,1,1]{1,0,5,4,3,2:T(4,128)} %constant.148, f32[4,4,4,8,8,128]{5,4,3,2,1,0:T(8,128)S(1)} %bitcast.101), kind=kOutput, calls=%fused_computation.25 | convolution fusion | flops 25165824 | bytes 4194368 | tf_op jit(solution)/shard_map/abcdef,zb->azcdef/dot_general | solution.py:120
  6.6 4.5 %fusion.24 = f32[4,4,4,8,8,128]{5,2,4,3,1,0:T(4,128)S(1)} fusion(f32[4,4,1,1,1,1]{1,0,5,4,3,2:T(4,128)S(1)} %copy-done.9, f32[4,4,4,8,8,128]{5,1,4,3,2,0:T(4,128)S(1)} %fusion.21), kind=kOutput, calls=%fused_computation.26 | convolution fusion | flops 25165824 | bytes 4194368 | tf_op jit(solution)/shard_map/abcdef,zc->abzdef/dot_general | solution.py:120
  11.2 3.0 %fusion.27 = f32[4,4,4,8,8,128]{5,3,4,2,1,0:T(8,128)S(1)} fusion(f32[8,8,1,1,1,1]{1,0,5,4,3,2:T(8,128)S(1)} %copy-done.7, f32[4,4,4,8,8,128]{5,2,4,3,1,0:T(4,128)S(1)} %fusion.24), kind=kOutput, calls=%fused_computation.27 | convolution fusion | flops 50331648 | bytes 4194560 | tf_op jit(solution)/shard_map/abcdef,zd->abczef/dot_general | solution.py:120
  14.2 2.1 fusion.13
  16.3 1.9 fusion.7
  18.3 1.3 copy-done.1
  19.6 2.5 %stack.3 = f32[8,1,4,4,8,8,128]{6,5,4,3,2,1,0:T(8,128)} broadcast(f32[4,4,8,8,128]{4,3,2,1,0:T(8,128)S(1)} %slice_bitcast_fusion), dimensions={2,3,4,5,6} | broadcast | bytes 4718592 | tf_op jit(solution)/shard_map/stack | solution.py:152
  22.1 8.3 %all-to-all-start = ((f32[8,1,4,4,8,8,128]{6,5,4,3,2,1,0:T(8,128)}), f32[8,1,4,4,8,8,128]{6,5,4,3,2,1,0:T(8,128)}, u32[]{:S(2)}, u32[]{:S(2)}) async-start(f32[8,1,4,4,8,8,128]{6,5,4,3,2,1,0:T(8,128)} %stack.3), calls=%async_computation | async-start | bytes 8388608 | tf_op jit(solution)/shard_map/all_to_all | solution.py:152
  31.1 0.7 fusion.40
  35.9 53.5 %all-to-all-done = f32[8,1,4,4,8,8,128]{6,5,4,3,2,1,0:T(8,128)} async-done(((f32[8,1,4,4,8,8,128]{6,5,4,3,2,1,0:T(8,128)}), f32[8,1,4,4,8,8,128]{6,5,4,3,2,1,0:T(8,128)}, u32[]{:S(2)}, u32[]{:S(2)}) %all-to-all-start) | async-done | bytes 4194336 | tf_op jit(solution)/shard_map/all_to_all | solution.py:152
  89.4 8.1 %fusion = f32[4,4,8,8,128,8]{4,5,3,2,1,0:T(8,128)S(1)} fusion(f32[8,8,1,1,1,1]{1,0,5,4,3,2:T(8,128)S(1)} %copy-done.11, f32[8,1,4,4,8,8,128]{6,5,4,3,2,1,0:T(8,128)} %all-to-all-done), kind=kOutput, calls=%fused_computation | convolution fusion | flops 100663296 | bytes 8388864 | tf_op jit(solution)/shard_map/abcdef,za->zbcdef/dot_general | solution.py:120
  97.6 0.6 dynamic-slice_bitcast_fusion
  98.1 1.1 dynamic-slice_bitcast_fusion.1
  99.3 5.4 %multiply_add_fusion = f32[4,4,4,8,8,128]{5,0,4,3,2,1:T(4,128)} fusion(f32[4,4,1,1,1,1]{1,0,5,4,3,2:T(4,128)S(1)} %copy-done.13, f32[4,4,4,8,8,128]{5,4,3,2,1,0:T(8,128)S(1)} %copy-done.2, f32[4,4,8,8,128]{4,3,2,1,0:T(8,128)S(1)} %dynamic-slice_bitcast_fusion.1, f32[4]{0:T(128)S(1)} %copy-done.15), kind=kOutput, calls=%fused_computation.24 | convolution fusion | flops 26214400 | bytes 4718672 | tf_op jit(solution)/shard_map/abcdef,za->zbcdef/dot_general | solution.py:120
  104.8 13.8 %scatter.6 = f32[4,4,4,8,8,128]{5,0,4,3,2,1:T(4,128)} dynamic-update-slice(f32[4,4,4,8,8,128]{5,0,4,3,2,1:T(4,128)} %multiply_add_fusion, f32[1,4,4,8,8,128]{5,0,4,3,2,1:T(1,128)S(1)} %dynamic-slice_bitcast_fusion, s32[]{:T(128)} %constant.124.clone.1, s32[]{:T(128)} %constant.124.clone.1, s32[]{:T(128)} %constant.124.clone.1, s32[]{:T(128)} %constant.124.clone.1, s32[]{:T(128)} %constant.124.clone.1, ...) | dynamic-update-slice | bytes 1048580 | tf_op jit(solution)/shard_map/scatter | solution.py:163
  118.6 2.3 fusion.3
  120.9 32.9 %all_to_all.15 = f32[16,4,1,8,8,128]{5,1,4,3,2,0:T(4,128)S(1)} all-to-all(f32[16,4,1,8,8,128]{5,1,4,3,2,0:T(4,128)S(1)} %bitcast.102), channel_id=1, replica_groups=mesh['grid'=16,'dom'=8] {'grid'}, dimensions={0} | all-to-all | bytes 4194304 | tf_op jit(solution)/shard_map/all_to_all | solution.py:17
  155.3 28.2 %all-gather = f32[8,8,8,128]{3,2,1,0:T(8,128)S(1)} all-gather(f32[1,8,8,128]{3,2,1,0:T(8,128)S(1)} %slice.118), channel_id=2, replica_groups=mesh['grid'=16,'dom'=8] {'dom'}, dimensions={0}, use_global_device_ids=true | all-gather | bytes 294912 | tf_op jit(solution)/shard_map/all_gather | solution.py:170
  184.8 36.6 %all_to_all.16 = f32[16,4,1,8,8,128]{5,4,3,1,2,0:T(8,128)S(1)} all-to-all(f32[16,4,1,8,8,128]{5,4,3,1,2,0:T(8,128)S(1)} %broadcast_in_dim.4), channel_id=1, replica_groups=mesh['grid'=16,'dom'=8] {'grid'}, dimensions={0} | all-to-all | bytes 4194304 | tf_op jit(solution)/shard_map/all_to_all | solution.py:29
  221.5 4.3 %fusion.32 = f32[4,4,4,8,8,128]{5,1,4,3,2,0:T(4,128)S(1)} fusion(f32[4,4,1,1,1,1]{1,0,5,4,3,2:T(4,128)S(1)} %copy-done.8, f32[4,4,4,8,8,128]{5,4,3,0,2,1:T(8,128)S(1)} %bitcast.103), kind=kOutput, calls=%fused_computation.28 | convolution fusion | flops 25165824 | bytes 4194368 | tf_op jit(solution)/shard_map/abcdef,zb->azcdef/dot_general | solution.py:120
  225.8 4.3 %fusion.9 = f32[4,4,8,8,128,4]{4,5,3,2,1,0:T(4,128)S(1)} fusion(f32[4,4,1,1,1,1]{1,0,5,4,3,2:T(4,128)S(1)} %copy-done.8, f32[4,4,4,8,8,128]{5,1,4,3,2,0:T(4,128)S(1)} %fusion.32), kind=kOutput, calls=%fused_computation.12 | convolution fusion | flops 25165824 | bytes 4194368 | tf_op jit(solution)/shard_map/abcdef,zc->abzdef/dot_general | solution.py:120
  230.1 1.6 fusion.4
  231.8 1.6 copy.88
  (47 shorter events, 3.2 us)
Async XLA Ops:
  0.0 1.6 copy-start
  1.6 5.0 %copy-start.9 = (f32[4,4,1,1,1,1]{1,0,5,4,3,2:T(4,128)S(1)}, f32[4,4,1,1,1,1]{1,0,5,4,3,2:T(4,128)}, u32[]{:S(2)}) copy-start(f32[4,4,1,1,1,1]{1,0,5,4,3,2:T(4,128)} %constant.148) | copy-start | bytes 196
  6.6 4.5 %copy-start.7 = (f32[8,8,1,1,1,1]{1,0,5,4,3,2:T(8,128)S(1)}, f32[8,8,1,1,1,1]{1,0,5,4,3,2:T(8,128)}, u32[]{:S(2)}) copy-start(f32[8,8,1,1,1,1]{1,0,5,4,3,2:T(8,128)} %constant.149) | copy-start | bytes 772
  14.2 2.1 copy-start.3
  18.3 1.3 copy-start.1
  22.1 8.9 %copy-start.5 = (s32[1,6]{1,0:T(1,128)S(1)}, s32[1,6]{1,0:T(1,128)}, u32[]{:S(2)}) copy-start(s32[1,6]{1,0:T(1,128)} %param.24) | copy-start | bytes 76
  22.1 67.3 %copy-start.11 = (f32[8,8,1,1,1,1]{1,0,5,4,3,2:T(8,128)S(1)}, f32[8,8,1,1,1,1]{1,0,5,4,3,2:T(8,128)}, u32[]{:S(2)}) copy-start(f32[8,8,1,1,1,1]{1,0,5,4,3,2:T(8,128)} %constant.151) | copy-start | bytes 772
  22.1 67.3 %all-to-all-start = ((f32[8,1,4,4,8,8,128]{6,5,4,3,2,1,0:T(8,128)}), f32[8,1,4,4,8,8,128]{6,5,4,3,2,1,0:T(8,128)}, u32[]{:S(2)}, u32[]{:S(2)}) async-start(f32[8,1,4,4,8,8,128]{6,5,4,3,2,1,0:T(8,128)} %stack.3), calls=%async_computation | async-start | bytes 8388608 | tf_op jit(solution)/shard_map/all_to_all | solution.py:152
  89.4 9.9 %copy-start.13 = (f32[4,4,1,1,1,1]{1,0,5,4,3,2:T(4,128)S(1)}, f32[4,4,1,1,1,1]{1,0,5,4,3,2:T(4,128)}, u32[]{:S(2)}) copy-start(f32[4,4,1,1,1,1]{1,0,5,4,3,2:T(4,128)} %constant.147) | copy-start | bytes 196
  97.5 1.7 copy-start.2
  97.6 1.7 copy-start.15
  153.8 0.7 copy-start.6
  153.8 1.3 copy-start.4
  153.8 29.7 %copy-start.10 = (f32[8,8,1,1]{1,0,3,2:T(8,128)S(1)}, f32[8,8,1,1]{1,0,3,2:T(8,128)}, u32[]{:S(2)}) copy-start(f32[8,8,1,1]{1,0,3,2:T(8,128)} %constant.153) | copy-start | bytes 772
  153.8 30.3 %copy-start.12 = (f32[4,4,1,1]{1,0,3,2:T(4,128)S(1)}, f32[4,4,1,1]{1,0,3,2:T(4,128)}, u32[]{:S(2)}) copy-start(f32[4,4,1,1]{1,0,3,2:T(4,128)} %constant.145) | copy-start | bytes 196
  153.8 30.3 %copy-start.14 = (f32[4]{0:T(128)S(1)}, f32[4]{0:T(128)}, u32[]{:S(2)}) copy-start(f32[4]{0:T(128)} %constant.140.clone) | copy-start | bytes 52
  184.8 36.6 %copy-start.8 = (f32[4,4,1,1,1,1]{1,0,5,4,3,2:T(4,128)S(1)}, f32[4,4,1,1,1,1]{1,0,5,4,3,2:T(4,128)}, u32[]{:S(2)}) copy-start(f32[4,4,1,1,1,1]{1,0,5,4,3,2:T(4,128)} %constant.154) | copy-start | bytes 196
